TPU v7x, 512 devices: a whole 4x8x8 slice. The times are simulated.
512 devices in a mesh: chan: 64 (over y_hi, z, core), tm: 8 (over x, y_lo).
Axes of the slice: x: 4, y: 8 (y_hi: 4, y_lo: 2; y = y_hi * 2 + y_lo), z: 8, core: 2. Of those that a mesh axis runs over, the one named last changes fastest.
Arguments:
- voltages: bfloat16 [2, 512, 256, 2048], P(None, None, 'chan', 'tm'), may hold values from -6 to 6, as said below
- flag_mask: int32 [16, 256], P('tm', 'chan'), may hold values from 0 to 1, as said below
- flagged_prefix_counts: int32 [16, 256], P('tm', 'chan'), may hold values from 0 to 127
Outputs:
- visibilities: float32 [512, 2, 256, 256], P(('chan', 'tm'))
Inputs may be any that keep to these rules, and one draw needn't show every extreme that they name: `voltages`: samples that keep drops count as zero; a program may move only the kept samples, in any compact form. `flag_mask`: 1 keeps the block of 128 samples of an antenna, 0 drops it; some antennas are dropped in every block. The first flagged_prefix_counts samples of a kept block are flagged; flags and counts may be packed several to a word wherever they are moved.
All inputs are finite; a program needn't handle non-finite values.
Results may differ from a plain program's by a relative error of at most 0.0003.
Values may be sent and summed in bfloat16 or wider, within the bound.
No kernel may reach another device: no remote copies, remote signals or barrier semaphores. Data moves between devices by JAX's collectives and lax.ppermute only.
A program may use at most 64 MiB of HBM per device.

v0:
```python
import jax
import jax.numpy as jnp
from jax import lax
from jax.sharding import PartitionSpec as P

FLAG_BLOCK_WIDTH = 128


def joined_along(blocks, dim):
    blocks = jnp.moveaxis(blocks, 0, dim)
    dims = blocks.shape
    return blocks.reshape(*dims[:dim], dims[dim] * dims[dim + 1], *dims[dim + 2 :])


def gather_together(arrays, axis, dims):
    line = jnp.concatenate([a.reshape(-1) for a in arrays])
    lines, at, finished = (lax.all_gather(line, axis), 0, [])
    for a, dim in zip(arrays, dims):
        blocks = lines[:, at : at + a.size].reshape(-1, *a.shape)
        finished.append(joined_along(blocks, dim))
        at += a.size
    return tuple(finished)


def split_up(x, dim, length):
    before, after = (x.shape[:dim], x.shape[dim + 1 :])
    return jnp.moveaxis(x.reshape(*before, length, -1, *after), dim, 0)


def one_exchange(x, axis, axes, splits, concats):
    sizes = [lax.axis_size(a) for a in axes]
    blocks = split_up(x, splits[0], sizes[0])
    blocks = jnp.moveaxis(split_up(blocks, splits[1] + 1, sizes[1]), 0, 1)
    inside = blocks.shape[2:]
    blocks = blocks.reshape(-1, *inside)
    blocks = lax.all_to_all(blocks, axis, split_axis=0, concat_axis=0, tiled=True)
    blocks = joined_along(blocks.reshape(*sizes, *inside), concats[0] + 1)
    return joined_along(blocks, concats[1])


def pair_samples(flag_mask, flagged_prefix_counts):

    def add_block(total, block):
        live = block[0].astype(jnp.float32)
        cover = (FLAG_BLOCK_WIDTH - jnp.maximum(block[1][:, None], block[1][None, :])).astype(
            jnp.float32
        )
        return (total + live[:, None] * live[None, :] * cover, 0)

    start = jnp.zeros((flag_mask.shape[1], flag_mask.shape[1]), jnp.float32)
    total, unused = lax.scan(add_block, start, (flag_mask, flagged_prefix_counts))
    return total


def cross_products(slab):
    real_part, imag_part = (slab[0], slab[1])
    rr = jnp.einsum("cit,cjt->cij", real_part, real_part, preferred_element_type=jnp.float32)
    ii = jnp.einsum("cit,cjt->cij", imag_part, imag_part, preferred_element_type=jnp.float32)
    ir = jnp.einsum("cit,cjt->cij", imag_part, real_part, preferred_element_type=jnp.float32)
    ri = jnp.einsum("cit,cjt->cij", real_part, imag_part, preferred_element_type=jnp.float32)
    real_out = rr + ii
    imag_out = ir - ri
    return jnp.stack([real_out, imag_out], axis=1)


def arrange_flags(gathered, chan_devices, time_devices):
    blocks_here = gathered.shape[1]
    antennas_here = gathered.shape[2]
    grid = gathered.reshape(chan_devices, time_devices, blocks_here, antennas_here)
    grid = grid.transpose(1, 2, 0, 3)
    return grid.reshape(time_devices * blocks_here, chan_devices * antennas_here)


def shards(voltages, flag_mask, flagged_prefix_counts):
    antenna_slice = voltages.shape[2]
    sample_slice = voltages.shape[3]
    offsets = jnp.arange(FLAG_BLOCK_WIDTH, dtype=jnp.int32)
    retain_mask = (flag_mask.T[:, :, None] == 1) & (
        offsets[None, None, :] >= flagged_prefix_counts.T[:, :, None]
    )
    retain_mask = retain_mask.reshape(antenna_slice, sample_slice)
    masked = jnp.where(retain_mask[None, None], voltages, jnp.zeros((), voltages.dtype))
    mask_pieces, count_pieces = gather_together(
        (flag_mask[None], flagged_prefix_counts[None]), ("chan", "tm"), (0, 0)
    )
    chan_devices = lax.axis_size("chan")
    time_devices = lax.axis_size("tm")
    all_mask = arrange_flags(mask_pieces, chan_devices, time_devices)
    all_counts = arrange_flags(count_pieces, chan_devices, time_devices)
    pairs = pair_samples(all_mask, all_counts)
    turned = one_exchange(masked, ("chan", "tm"), ("chan", "tm"), (1, 1), (2, 3))
    summed = cross_products(turned)
    return summed / jnp.maximum(pairs, 1.0)[None, None]


def solution(mesh):
    placed = (P(None, None, "chan", "tm"), P("tm", "chan"), P("tm", "chan"))
    return jax.shard_map(
        shards,
        mesh=mesh,
        in_specs=placed,
        out_specs=P(("chan", "tm"), None, None, None),
        check_vma=False,
    )
```

profile of v0, /device:TPU:26, one launch (start us, length us, event | category | flops | bytes accessed | tf_op | source)
XLA Modules:
  0.0 180.6 jit_solution(4875701789765785955)
XLA Ops:
  0.0 0.8 copy.13
  0.8 0.7 compare_bitcast_fusion
  1.6 2.4 %broadcast_select_fusion = bf16[2,512,4,256]{3,2,1,0:T(4,128)(2,1)S(1)} fusion(bf16[2,512,4,256]{3,2,1,0:T(4,128)(2,1)} %param.5, pred[4,256]{1,0:T(4,128)(4,1)S(1)} %fusion.4), kind=kLoop, calls=%fused_computation.4 | loop fusion | flops 1048576 | bytes 4195328 | tf_op jit(solution)/shard_map/jit(_where)/select_n | solution.py:82
  4.0 2.3 %copy.14 = bf16[2,64,8,4,256]{4,3,0,2,1:T(4,128)(2,1)} copy(bf16[2,64,8,4,256]{4,3,2,1,0:T(4,128)(2,1)S(1)} %bitcast.75) | data formatting | bytes 4194304 | tf_op jit(solution)/shard_map/reshape | solution.py:27
  6.3 20.9 %all-to-all-start = ((bf16[512,2,1,4,256]{4,3,1,2,0:T(4,128)(2,1)}), bf16[512,2,1,4,256]{4,3,1,2,0:T(4,128)(2,1)S(1)}, u32[]{:S(2)}, u32[]{:S(2)}) async-start(bf16[512,2,1,4,256]{4,3,1,2,0:T(4,128)(2,1)} %bitcast.76), calls=%async_computation | async-start | bytes 4194304 | tf_op jit(solution)/shard_map/all_to_all | solution.py:36
  27.4 0.2 add_dynamic-update-slice_fusion
  27.6 138.0 %all-reduce = s32[8192]{0:T(1024)S(1)} all-reduce(s32[8192]{0:T(1024)S(1)} %add_dynamic-update-slice_fusion), channel_id=2, replica_groups=mesh['chan'=64,'tm'=8] {'chan','tm'}, use_global_device_ids=true, to_apply=%add | all-reduce | flops 8192 | bytes 65536
  166.0 0.2 reshape_reshape_reshape.6
  166.2 0.9 copy.18
  167.0 0.3 reshape.145
  167.4 0.2 reshape_reshape_reshape.7
  167.6 0.9 copy.20
  168.4 0.3 reshape.146
  168.7 3.2 %while.11 = (s32[]{:T(128)}, f32[256,256]{1,0:T(8,128)S(1)}, s32[16,256]{1,0:T(8,128)S(1)}, s32[16,256]{1,0:T(8,128)S(1)}, s32[]{:T(128)}, /*index=5*/s32[]{:T(128)}) while((s32[]{:T(128)}, f32[256,256]{1,0:T(8,128)S(1)}, s32[16,256]{1,0:T(8,128)S(1)}, s32[16,256]{1,0:T(8,128)S(1)}, s32[]{:T(128)}, /*index=5*/s32[]{:T(128)}) %tuple.26), condition=%wide.region_1.2_spmd.clone, body=%wide.region_0.1_spmd.clone.sunk | while | flops 459011 | bytes 530515 | solution.py:51
  169.0 0.2 select_add_fusion.2
  169.2 0.2 select_add_fusion.2
  172.0 0.4 copy.26
  172.4 1.6 copy.16
  174.0 2.1 %reshape.142 = bf16[8,2,1,256,256]{4,3,0,2,1:T(8,128)(2,1)} reshape(bf16[8,2,1,64,4,256]{5,4,3,0,1,2:T(4,128)(2,1)S(1)} %copy.16) | data formatting | bytes 4194304 | tf_op jit(solution)/shard_map/reshape | solution.py:12
  176.1 2.2 %convolution_bitcast_fusion.2 = f32[256,256]{1,0:T(8,128)S(1)} fusion(bf16[2,1,256,8,256]{4,2,3,1,0:T(8,128)(2,1)} %bitcast.78), kind=kOutput, calls=%fused_computation.7 | convolution fusion | flops 268435456 | bytes 1310720 | tf_op jit(solution)/shard_map/cit,cjt->cij/dot_general | solution.py:58
  178.4 0.5 convolution_bitcast_fusion
  178.8 0.5 fusion.1
  179.3 0.5 fusion.3
  179.8 0.8 maximum_divide_fusion
  (49 shorter events, 3.1 us)
Async XLA Ops:
  6.3 20.9 %copy-start.2 = (s32[2,4]{1,0:T(2,128)S(1)}, s32[2,4]{1,0:T(2,128)}, u32[]{:S(2)}) copy-start(s32[2,4]{1,0:T(2,128)} %param.6) | copy-start | bytes 100
  6.3 21.0 %copy-start.1 = (s32[2,4]{1,0:T(2,128)S(1)}, s32[2,4]{1,0:T(2,128)}, u32[]{:S(2)}) copy-start(s32[2,4]{1,0:T(2,128)} %param.7) | copy-start | bytes 100
  6.3 165.6 %all-to-all-start = ((bf16[512,2,1,4,256]{4,3,1,2,0:T(4,128)(2,1)}), bf16[512,2,1,4,256]{4,3,1,2,0:T(4,128)(2,1)S(1)}, u32[]{:S(2)}, u32[]{:S(2)}) async-start(bf16[512,2,1,4,256]{4,3,1,2,0:T(4,128)(2,1)} %bitcast.76), calls=%async_computation | async-start | bytes 4194304 | tf_op jit(solution)/shard_map/all_to_all | solution.py:36
  176.1 2.2 %copy-start = (bf16[8,2,1,256,256]{4,3,0,2,1:T(8,128)(2,1)S(1)}, bf16[8,2,1,256,256]{4,3,0,2,1:T(8,128)(2,1)}, u32[]{:S(2)}) copy-start(bf16[8,2,1,256,256]{4,3,0,2,1:T(8,128)(2,1)} %reshape.142) | copy-start | bytes 6291460
where the time goes:
time: 181 us
  blocking collectives  138 us (76%)
  starting transfers between devices  20.9 us (12%)
  local copies, waits for them, and re-layouts  10.5 us (6%)
  other arithmetic  6.84 us (4%)
  matrix products  3.63 us (2%)
    unnamed x1, blocking collectives  138 us
    all_to_all x1, starting transfers between devices, one_exchange(): lax.all_to_all(blocks, axis, split_axis=0, concat_axis=0, tiled=True)  20.9 us
  transfers between devices with their start and end apart: 1, of which 0 were waited for; matrix products, arithmetic and copies ran while one was open for 3% of the time, Pallas kernels for 0%

commit v1 on v0

v1 whole, which is shorter than its diff:
```python
import jax
import jax.numpy as jnp
from jax import lax
from jax.sharding import PartitionSpec as P

FLAG_BLOCK_WIDTH = 128
CODE_FLOOR = 8.0
CODE_BASE = 16.0


def first_kept(flag_mask, flagged_prefix_counts):
    return jnp.where(flag_mask == 1, flagged_prefix_counts, FLAG_BLOCK_WIDTH)


def shards(voltages, flag_mask, flagged_prefix_counts):
    parts, channels, ants, times = voltages.shape
    blocks = times // FLAG_BLOCK_WIDTH
    chan_devices = lax.axis_size("chan")
    time_devices = lax.axis_size("tm")
    first = first_kept(flag_mask, flagged_prefix_counts).T
    code = jnp.where(first > 0, first.astype(jnp.float32) + CODE_BASE, 0.0)
    code = code.astype(jnp.bfloat16)
    lane = jnp.arange(times, dtype=jnp.int32)
    code_line = jnp.repeat(code, FLAG_BLOCK_WIDTH, axis=1)
    put = (lane[None, :] % FLAG_BLOCK_WIDTH == 0) & (code_line > 0)
    real_part = jnp.where(put[None], code_line[None], voltages[0])
    line = jnp.stack([real_part, voltages[1]], axis=1)
    line = lax.all_to_all(line, ("chan", "tm"), 0, 0, tiled=True)
    line = line.reshape(chan_devices, time_devices, parts, ants, times)
    line = line.transpose(2, 0, 3, 1, 4).reshape(
        parts, chan_devices * ants, time_devices * blocks, FLAG_BLOCK_WIDTH
    )
    heads = line[0, :, :, 0].astype(jnp.float32)
    first = jnp.where(heads > CODE_FLOOR, heads - CODE_BASE, 0.0).astype(jnp.int32)
    offsets = jnp.arange(FLAG_BLOCK_WIDTH, dtype=jnp.int32)
    keep = (offsets >= first[:, :, None]).reshape(chan_devices * ants, -1)
    line = line.reshape(parts, chan_devices * ants, -1)
    line = jnp.where(keep[None], line, jnp.zeros((), line.dtype))
    keep = keep.astype(jnp.bfloat16)

    def gram(a, b):
        return jnp.einsum("it,jt->ij", a, b, preferred_element_type=jnp.float32)

    pairs = jnp.maximum(gram(keep, keep), 1.0)
    real_out = gram(line[0], line[0]) + gram(line[1], line[1])
    cross = gram(line[1], line[0])
    imag_out = cross - cross.T
    return (jnp.stack([real_out, imag_out]) / pairs[None])[None]


def solution(mesh):
    placed = (P(None, None, "chan", "tm"), P("tm", "chan"), P("tm", "chan"))
    return jax.shard_map(
        shards,
        mesh=mesh,
        in_specs=placed,
        out_specs=P(("chan", "tm"), None, None, None),
        check_vma=False,
    )
```

time: 181 us -> 99.9 us (0.55)
  the two profiles are of different devices: /device:TPU:26 before, /device:TPU:2 now
where the time goes in v1:
time: 99.9 us; the launch traced here: 99.7 us
  waiting for transfers between devices  55 us (55%)
  starting transfers between devices  21.2 us (21%)
  local copies, waits for them, and re-layouts  13.8 us (14%)
  other arithmetic  5.65 us (6%)
  matrix products  3.88 us (4%)
    all_to_all x1, waiting for transfers between devices, shards(): line = lax.all_to_all(line, ('chan', 'tm'), 0, 0, tiled=True)  55 us
    all_to_all x1, starting transfers between devices, shards(): line = lax.all_to_all(line, ('chan', 'tm'), 0, 0, tiled=True)  21.2 us
    dot_general x4, matrix products, gram(): return jnp.einsum('it,jt->ij', a, b, preferred_element_type=jnp.float32)  3.88 us
    unnamed x11, local copies, waits for them, and re-layouts  2.7 us
    another operation x1, other arithmetic, shards(): line = jnp.stack([real_part, voltages[1]], axis=1)  2.69 us
    another operation x1, local copies, waits for them, and re-layouts, shards(): line = line.reshape(parts, chan_devices * ants, -1)  2.32 us
    reshape x1, local copies, waits for them, and re-layouts, shards(): line = line.reshape(chan_devices, time_devices, parts, ants, times)  2.19 us
    reshape x1, local copies, waits for them, and re-layouts, shards(): line.transpose(2, 0, 3, 1, 4)  2.15 us
  transfers between devices with their start and end apart: 1, of which 1 were waited for; matrix products, arithmetic and copies ran while one was open for 0% of the time, Pallas kernels for 0%

profile of v1, /device:TPU:2, one launch (start us, length us, event | category | flops | bytes accessed | tf_op | source)
XLA Modules:
  0.0 99.7 jit_solution(11297205802765697409)
XLA Ops:
  0.0 0.9 fusion.13
  0.9 0.1 copy.27
  1.0 0.1 broadcast_bitcast_fusion
  1.1 1.6 %slice_bitcast_fusion.2 = bf16[512,1,4,256]{3,2,1,0:T(4,128)(2,1)S(1)} fusion(bf16[2,512,4,256]{3,2,1,0:T(4,128)(2,1)} %param.3), kind=kLoop, calls=%fused_computation.14 | loop fusion | bytes 2097152 | tf_op jit(solution)/shard_map/stack;squeeze | solution.py:27
  2.7 0.4 bitcast_select_fusion
  3.1 2.7 %pad_maximum_fusion = bf16[512,2,4,256]{3,2,1,0:T(4,128)(2,1)} fusion(bf16[512,1,4,256]{3,2,1,0:T(4,128)(2,1)S(1)} %slice_bitcast_fusion.2, bf16[512,1,4,256]{3,2,1,0:T(4,128)(2,1)S(1)} %bitcast_select_fusion), kind=kLoop, calls=%fused_computation | loop fusion | flops 1048576 | bytes 4194304 | tf_op jit(solution)/shard_map/stack | solution.py:27
  5.8 21.2 %all-to-all-start = ((bf16[512,2,4,256]{3,2,1,0:T(4,128)(2,1)}), bf16[512,2,4,256]{3,2,1,0:T(4,128)(2,1)S(1)}, u32[]{:S(2)}, u32[]{:S(2)}) async-start(bf16[512,2,4,256]{3,2,1,0:T(4,128)(2,1)} %pad_maximum_fusion), calls=%async_computation | async-start | bytes 4194304 | tf_op jit(solution)/shard_map/all_to_all | solution.py:28
  27.0 55.0 %all-to-all-done = bf16[512,2,4,256]{3,2,1,0:T(4,128)(2,1)S(1)} async-done(((bf16[512,2,4,256]{3,2,1,0:T(4,128)(2,1)}), bf16[512,2,4,256]{3,2,1,0:T(4,128)(2,1)S(1)}, u32[]{:S(2)}, u32[]{:S(2)}) %all-to-all-start) | async-done | bytes 2097184 | tf_op jit(solution)/shard_map/all_to_all | solution.py:28
  82.1 1.3 %copy-done.1 = bf16[512,2,4,256]{3,2,1,0:T(4,128)(2,1)} copy-done((bf16[512,2,4,256]{3,2,1,0:T(4,128)(2,1)}, bf16[512,2,4,256]{3,2,1,0:T(4,128)(2,1)S(1)}, u32[]{:S(2)}) %copy-start.1) | copy-done | bytes 2097176
  83.4 2.2 %copy.42 = bf16[64,8,2,4,256]{4,1,3,0,2:T(8,128)(2,1)S(1)} copy(bf16[64,8,2,4,256]{4,3,2,1,0:T(4,128)(2,1)} %bitcast.49) | data formatting | bytes 4194304 | tf_op jit(solution)/shard_map/reshape | solution.py:29
  85.6 2.2 %reshape.128 = bf16[2,256,16,128]{3,2,1,0:T(8,128)(2,1)} reshape(bf16[2,64,4,8,256]{4,3,2,1,0:T(8,128)(2,1)S(1)} %bitcast.47) | data formatting | bytes 4194304 | tf_op jit(solution)/shard_map/reshape | solution.py:30
  87.7 2.3 %reshape_reshape.3 = bf16[2,256,2048]{2,1,0:T(8,128)(2,1)} reshape(bf16[2,64,4,8,256]{4,3,2,1,0:T(8,128)(2,1)S(1)} %bitcast.48) | data formatting | bytes 4194304 | tf_op jit(solution)/shard_map/reshape;reshape | solution.py:37
  90.1 1.6 %slice.24 = bf16[1,256,16,1]{3,2,1,0:T(8,128)(2,1)S(1)} slice(bf16[2,256,16,128]{3,2,1,0:T(8,128)(2,1)} %reshape.128), slice={[0:1], [0:256], [0:16], [0:1]} | slice | bytes 16384 | tf_op jit(solution)/shard_map/slice | solution.py:33
  91.6 0.9 copy.36
  92.5 0.5 bitcast_compare_fusion
  93.0 1.0 %copy.30 = pred[256,2048]{1,0:T(8,128)(4,1)S(1)} copy(pred[256,2048]{0,1:T(8,128)(4,1)S(1)} %bitcast_compare_fusion) | data formatting | bytes 1048576 | tf_op jit(solution)/shard_map/ge | solution.py:36
  94.0 0.3 broadcast_select_fusion
  94.4 0.5 fusion.5
  94.8 0.5 fusion.6
  95.3 0.4 copy-done.3
  95.7 0.8 fusion.2
  96.5 0.1 copy.31
  96.7 2.1 %fusion.3 = f32[1,1,256,256]{3,2,1,0:T(8,128)S(1)} fusion(f32[256,256]{1,0:T(8,128)S(1)} %fusion.6, bf16[2,256,2048]{2,1,0:T(8,128)(2,1)} %copy-done.3), kind=kOutput, calls=%fused_computation.9 | convolution fusion | flops 268500992 | bytes 1572864 | tf_op jit(solution)/shard_map/it,jt->ij/dot_general | solution.py:42
  98.8 0.8 maximum_divide_fusion
  (12 shorter events, 0.1 us)
Async XLA Ops:
  0.0 2.7 %copy-start.2 = (bf16[2,512,4,256]{3,2,1,0:T(4,128)(2,1)S(1)}, bf16[2,512,4,256]{3,2,1,0:T(4,128)(2,1)}, u32[]{:S(2)}) copy-start(bf16[2,512,4,256]{3,2,1,0:T(4,128)(2,1)} %param.3) | copy-start | bytes 6291460
  5.8 76.3 %all-to-all-start = ((bf16[512,2,4,256]{3,2,1,0:T(4,128)(2,1)}), bf16[512,2,4,256]{3,2,1,0:T(4,128)(2,1)S(1)}, u32[]{:S(2)}, u32[]{:S(2)}) async-start(bf16[512,2,4,256]{3,2,1,0:T(4,128)(2,1)} %pad_maximum_fusion), calls=%async_computation | async-start | bytes 4194304 | tf_op jit(solution)/shard_map/all_to_all | solution.py:28
  82.0 1.3 %copy-start.1 = (bf16[512,2,4,256]{3,2,1,0:T(4,128)(2,1)}, bf16[512,2,4,256]{3,2,1,0:T(4,128)(2,1)S(1)}, u32[]{:S(2)}) copy-start(bf16[512,2,4,256]{3,2,1,0:T(4,128)(2,1)S(1)} %all-to-all-done) | copy-start | bytes 6291460
  90.0 4.0 %copy-start = (bf16[2,256,2048]{2,1,0:T(8,128)(2,1)S(1)}, bf16[2,256,2048]{2,1,0:T(8,128)(2,1)}, u32[]{:S(2)}) copy-start(bf16[2,256,2048]{2,1,0:T(8,128)(2,1)} %reshape_reshape.3) | copy-start | bytes 6291460
  94.4 1.3 %copy-start.3 = (bf16[2,256,2048]{2,1,0:T(8,128)(2,1)}, bf16[2,256,2048]{2,1,0:T(8,128)(2,1)S(1)}, u32[]{:S(2)}) copy-start(bf16[2,256,2048]{2,1,0:T(8,128)(2,1)S(1)} %broadcast_select_fusion) | copy-start | bytes 6291460

commit v2 on v1

v2 whole, which is shorter than its diff:
```python
import jax
import jax.numpy as jnp
from jax import lax
from jax.experimental import pallas as pl
from jax.experimental.pallas import tpu as pltpu
from jax.sharding import PartitionSpec as P

WIDTH = 128
CODE_FLOOR = 8.0
CODE_BASE = 16.0
PACK_STEPS = 8


def pack_kernel(mask_ref, count_ref, volt_ref, out_ref):
    parts, _, ants, times = volt_ref.shape
    blocks = times // WIDTH
    lane = lax.broadcasted_iota(jnp.int32, (ants, WIDTH), 1)
    row = lax.broadcasted_iota(jnp.int32, (ants, WIDTH), 0)
    for p in range(parts):
        for b in range(blocks):
            x = volt_ref[p, :, :, b * WIDTH : (b + 1) * WIDTH]
            if p == 0:
                code = jnp.zeros((ants, WIDTH), jnp.int32)
                for a in range(ants):
                    first = jnp.where(mask_ref[b, a] == 1, count_ref[b, a], WIDTH)
                    code = jnp.where(row == a, first, code)
                put = (lane == 0) & (code > 0)
                code = code.astype(jnp.float32) + CODE_BASE
                x = jnp.where(put[None], code[None], x.astype(jnp.float32)).astype(x.dtype)
            at = (p * blocks + b) * ants
            out_ref[:, at : at + ants, :] = x


def pack(voltages, flag_mask, counts):
    parts, channels, ants, times = voltages.shape
    step = channels // PACK_STEPS
    rows = parts * ants * times // WIDTH
    return pl.pallas_call(
        pack_kernel,
        grid=(PACK_STEPS,),
        in_specs=[
            pl.BlockSpec(memory_space=pltpu.SMEM),
            pl.BlockSpec(memory_space=pltpu.SMEM),
            pl.BlockSpec((parts, step, ants, times), lambda i: (0, i, 0, 0)),
        ],
        out_specs=pl.BlockSpec((step, rows, WIDTH), lambda i: (i, 0, 0)),
        out_shape=jax.ShapeDtypeStruct((channels, rows, WIDTH), voltages.dtype),
        name="pack",
    )(flag_mask, counts, voltages)


def gram_kernel(line_ref, out_ref, volt_scr, keep_scr, *, blocks):
    groups, rows, _ = line_ref.shape[0], line_ref.shape[2], WIDTH
    t = pl.program_id(0)
    ants = rows // (2 * blocks)
    all_ants = groups * ants
    lane = lax.broadcasted_iota(jnp.int32, (all_ants, WIDTH), 1).astype(jnp.float32)
    x = line_ref[:, 0].astype(jnp.float32)
    for b in range(blocks):
        re = x[:, b * ants : (b + 1) * ants].reshape(all_ants, WIDTH)
        at = (blocks + b) * ants
        im = x[:, at : at + ants].reshape(all_ants, WIDTH)
        head = re[:, 0:1]
        first = jnp.where(head > CODE_FLOOR, head - CODE_BASE, 0.0)
        keep = lane >= first
        slot = t * blocks + b
        volt_scr[0, slot] = jnp.where(keep, re, 0.0).astype(volt_scr.dtype)
        volt_scr[1, slot] = jnp.where(keep, im, 0.0).astype(volt_scr.dtype)
        keep_scr[slot] = jnp.where(keep, 1.0, 0.0).astype(keep_scr.dtype)

    @pl.when(t == pl.num_programs(0) - 1)
    def _():
        def dot(a, b):
            return lax.dot_general(a, b, (((1,), (1,)), ((), ())), preferred_element_type=jnp.float32)

        slots = volt_scr.shape[1]
        zero = jnp.zeros((all_ants, all_ants), jnp.float32)
        real_out, cross, pairs = zero, zero, zero
        for s in range(slots):
            re, im, keep = volt_scr[0, s], volt_scr[1, s], keep_scr[s]
            real_out = real_out + dot(re, re) + dot(im, im)
            cross = cross + dot(im, re)
            pairs = pairs + dot(keep, keep)
        pairs = jnp.maximum(pairs, 1.0)
        out_ref[0, 0] = real_out / pairs
        out_ref[0, 1] = (cross - cross.T) / pairs


def gram(line, time_devices, blocks, ants):
    groups = line.shape[0]
    rows = line.shape[2]
    all_ants = groups * ants
    slots = time_devices * blocks
    import functools

    return pl.pallas_call(
        functools.partial(gram_kernel, blocks=blocks),
        grid=(time_devices,),
        in_specs=[pl.BlockSpec((groups, 1, rows, WIDTH), lambda i: (0, i, 0, 0))],
        out_specs=pl.BlockSpec((1, 2, all_ants, all_ants), lambda i: (0, 0, 0, 0)),
        out_shape=jax.ShapeDtypeStruct((1, 2, all_ants, all_ants), jnp.float32),
        scratch_shapes=[
            pltpu.VMEM((2, slots, all_ants, WIDTH), jnp.bfloat16),
            pltpu.VMEM((slots, all_ants, WIDTH), jnp.bfloat16),
        ],
        name="gram",
    )(line)


def shards(voltages, flag_mask, flagged_prefix_counts):
    ants, times = voltages.shape[2:]
    chan_devices = lax.axis_size("chan")
    time_devices = lax.axis_size("tm")
    line = pack(voltages, flag_mask, flagged_prefix_counts)
    line = lax.all_to_all(line, ("chan", "tm"), 0, 0, tiled=True)
    line = line.reshape(chan_devices, time_devices, *line.shape[1:])
    return gram(line, time_devices, times // WIDTH, ants)


def solution(mesh):
    placed = (P(None, None, "chan", "tm"), P("tm", "chan"), P("tm", "chan"))
    return jax.shard_map(
        shards,
        mesh=mesh,
        in_specs=placed,
        out_specs=P(("chan", "tm"), None, None, None),
        check_vma=False,
    )
```

time: 99.9 us -> 90.9 us (0.910)
  blocking collectives: 0 us -> 76.4 us
  waiting for transfers between devices: 55 us -> 0 us
  starting transfers between devices: 21.2 us -> 0 us
  Pallas kernels: 0 us -> 14.2 us
  local copies, waits for them, and re-layouts: 13.8 us -> 0 us
  other arithmetic: 5.65 us -> 0 us
  matrix products: 3.88 us -> 0 us
    all_to_all x0 -> x1, blocking collectives: none -> 76.4 us  [shards(): line = lax.all_to_all(line, ('chan', 'tm'), 0, 0, tiled=True)]
    all_to_all x1 -> x0, waiting for transfers between devices: 55 us -> none  [shards(): line = lax.all_to_all(line, ('chan', 'tm'), 0, 0, tiled=True)]
    all_to_all x1 -> x0, starting transfers between devices: 21.2 us -> none  [shards(): line = lax.all_to_all(line, ('chan', 'tm'), 0, 0, tiled=True)]
    pallas_call x0 -> x2, Pallas kernels: none -> 14.2 us  [the longest x1 8.13 us: gram(): pl.pallas_call(functools.partial(gram_kernel, blocks=blocks), grid=(time_...]
    reshape x2 -> x0, local copies, waits for them, and re-layouts: 4.34 us -> none  [the longest x1 2.19 us: shards(): line = line.reshape(chan_devices, time_devices, parts, ants, times)]
    another operation x2 -> x0, local copies, waits for them, and re-layouts: 3.91 us -> none  [the longest x1 2.32 us: shards(): line = line.reshape(parts, chan_devices * ants, -1)]
    dot_general x4 -> x0, matrix products: 3.88 us -> none  [gram(): return jnp.einsum('it,jt->ij', a, b, preferred_element_type=jnp.float32)]
    another operation x2 -> x0, other arithmetic: 2.73 us -> none  [the longest x1 2.69 us: shards(): line = jnp.stack([real_part, voltages[1]], axis=1)]
  transfers between devices with their start and end apart: 1 -> 0, of which waited for: 1 -> 0; matrix products, arithmetic and copies ran while one was open for 0% -> 0% of each run, Pallas kernels for 0% -> 0%
where the time goes in v2:
time: 90.9 us; the launch traced here: 90.6 us
  blocking collectives  76.4 us (84%)
  Pallas kernels  14.2 us (16%)
    all_to_all x1, blocking collectives, shards(): line = lax.all_to_all(line, ('chan', 'tm'), 0, 0, tiled=True)  76.4 us
    pallas_call x1, Pallas kernels, gram(): pl.pallas_call(functools.partial(gram_kernel, blocks=blocks), grid=(time_...  8.13 us
    pallas_call x1, Pallas kernels, pack(): pl.pallas_call(pack_kernel, grid=(PACK_STEPS,), in_specs=[pl.BlockSpec(me...  6.07 us

profile of v2, /device:TPU:2, one launch (start us, length us, event | category | flops | bytes accessed | tf_op | source)
XLA Modules:
  0.0 90.6 jit_solution(14525408442350641280)
XLA Ops:
  0.0 6.1 %pack.1 = bf16[512,16,128]{2,1,0:T(8,128)(2,1)} custom-call(s32[2,4]{1,0:T(2,128)} %mask_ref.1, s32[2,4]{1,0:T(2,128)} %count_ref.1, bf16[2,512,4,256]{3,2,1,0:T(4,128)(2,1)} %volt_ref.1), custom_call_target="tpu_custom_call" | custom-call | tf_op jit(solution)/shard_map/pack/pallas_call | solution.py:38
  6.1 76.4 %all_to_all.5 = bf16[512,16,128]{2,1,0:T(8,128)(2,1)} all-to-all(bf16[512,16,128]{2,1,0:T(8,128)(2,1)} %pack.1), channel_id=1, replica_groups=mesh['chan'=64,'tm'=8] {'chan','tm'}, dimensions={0} | all-to-all | bytes 4194304 | tf_op jit(solution)/shard_map/all_to_all | solution.py:115
  82.4 8.1 %gram.1 = f32[1,2,256,256]{3,2,1,0:T(8,128)} custom-call(bf16[64,8,16,128]{3,2,1,0:T(8,128)(2,1)} %bitcast.1), custom_call_target="tpu_custom_call" | custom-call | tf_op jit(solution)/shard_map/gram/pallas_call | solution.py:96

commit v3 on v1

v3 whole, which is shorter than its diff:
```python
import jax
import jax.numpy as jnp
from jax import lax
from jax.experimental import pallas as pl
from jax.experimental.pallas import tpu as pltpu
from jax.sharding import PartitionSpec as P

WIDTH = 128
CODE_FLOOR = 8.0
CODE_BASE = 16.0
PACK_CHUNKS = 4


def pack_kernel(mask_ref, count_ref, volt_ref, out_ref, scr, in_sem, out_sem):
    parts, channels, ants, times = volt_ref.shape
    blocks = times // WIDTH
    step = channels // PACK_CHUNKS

    def into(c, p):
        at = pl.ds(c * step, step)
        return pltpu.make_async_copy(volt_ref.at[p, at], scr.at[at, p], in_sem.at[c, p])

    def out(c):
        at = pl.ds(c * step, step)
        return pltpu.make_async_copy(scr.at[at], out_ref.at[at], out_sem.at[c])

    for c in range(PACK_CHUNKS):
        for p in range(parts):
            into(c, p).start()
    lane = lax.broadcasted_iota(jnp.int32, (ants, WIDTH), 1)
    row = lax.broadcasted_iota(jnp.int32, (ants, WIDTH), 0)
    puts, codes = [], []
    for b in range(blocks):
        code = jnp.zeros((ants, WIDTH), jnp.int32)
        for a in range(ants):
            first = jnp.where(mask_ref[b, a] == 1, count_ref[b, a], WIDTH)
            code = jnp.where(row == a, first, code)
        put = jnp.where((lane == 0) & (code > 0), 1.0, 0.0).astype(jnp.bfloat16)
        puts.append(put)
        codes.append((code.astype(jnp.float32) + CODE_BASE).astype(jnp.bfloat16))
    for c in range(PACK_CHUNKS):
        for p in range(parts):
            into(c, p).wait()
        for b in range(blocks):
            at = (pl.ds(c * step, step), 0, slice(None), pl.ds(b * WIDTH, WIDTH))
            scr[at] = jnp.where(puts[b][None] > 0.5, codes[b][None], scr[at])
        out(c).start()
    for c in range(PACK_CHUNKS):
        out(c).wait()


def pack(voltages, flag_mask, counts):
    parts, channels, ants, times = voltages.shape
    shape = (channels, parts, ants, times)
    return pl.pallas_call(
        pack_kernel,
        in_specs=[
            pl.BlockSpec(memory_space=pltpu.SMEM),
            pl.BlockSpec(memory_space=pltpu.SMEM),
            pl.BlockSpec(memory_space=pl.ANY),
        ],
        out_specs=pl.BlockSpec(memory_space=pl.ANY),
        out_shape=jax.ShapeDtypeStruct(shape, voltages.dtype),
        scratch_shapes=[
            pltpu.VMEM(shape, voltages.dtype),
            pltpu.SemaphoreType.DMA((PACK_CHUNKS, parts)),
            pltpu.SemaphoreType.DMA((PACK_CHUNKS,)),
        ],
        name="pack",
    )(flag_mask, counts, voltages)


def gram_kernel(line_ref, out_ref, line_scr, volt_scr, keep_scr, sem):
    groups, times_devices, parts, ants, times = line_ref.shape
    blocks = times // WIDTH
    all_ants = groups * ants
    samples = times_devices * times

    def into(t):
        return pltpu.make_async_copy(line_ref.at[:, t], line_scr.at[t], sem.at[t])

    for t in range(times_devices):
        into(t).start()
    lane = lax.broadcasted_iota(jnp.int32, (all_ants, WIDTH), 1).astype(jnp.float32)
    for t in range(times_devices):
        into(t).wait()
        for b in range(blocks):
            def piece(p):
                x = line_scr[t, :, p, :, b * WIDTH : (b + 1) * WIDTH]
                return x.astype(jnp.float32).reshape(all_ants, WIDTH)

            re, im = piece(0), piece(1)
            head = re[:, 0:1]
            keep = lane >= jnp.where(head > CODE_FLOOR, head - CODE_BASE, 0.0)
            at = t * times + b * WIDTH
            end = at + WIDTH
            volt_scr[:, at:end] = jnp.where(keep, re, 0.0).astype(volt_scr.dtype)
            volt_scr[:, samples + at : samples + end] = jnp.where(keep, im, 0.0).astype(volt_scr.dtype)
            keep_scr[:, at:end] = jnp.where(keep, 1.0, 0.0).astype(keep_scr.dtype)

    def dot(a, b):
        return lax.dot_general(a, b, (((1,), (1,)), ((), ())), preferred_element_type=jnp.float32)

    both, keep = volt_scr[...], keep_scr[...]
    scale = 1.0 / jnp.maximum(dot(keep, keep), 1.0)
    out_ref[0, 0] = dot(both, both) * scale
    cross = dot(both[:, samples:], both[:, :samples])
    out_ref[0, 1] = (cross - cross.T) * scale


def gram(line):
    groups, time_devices, parts, ants, times = line.shape
    all_ants = groups * ants
    samples = time_devices * times
    return pl.pallas_call(
        gram_kernel,
        in_specs=[pl.BlockSpec(memory_space=pl.ANY)],
        out_specs=pl.BlockSpec(memory_space=pltpu.VMEM),
        out_shape=jax.ShapeDtypeStruct((1, 2, all_ants, all_ants), jnp.float32),
        scratch_shapes=[
            pltpu.VMEM((time_devices, groups, parts, ants, times), line.dtype),
            pltpu.VMEM((all_ants, parts * samples), line.dtype),
            pltpu.VMEM((all_ants, samples), line.dtype),
            pltpu.SemaphoreType.DMA((time_devices,)),
        ],
        name="gram",
    )(line)


def shards(voltages, flag_mask, flagged_prefix_counts):
    chan_devices = lax.axis_size("chan")
    time_devices = lax.axis_size("tm")
    line = pack(voltages, flag_mask, flagged_prefix_counts)
    line = lax.all_to_all(line, ("chan", "tm"), 0, 0, tiled=True)
    return gram(line.reshape(chan_devices, time_devices, *line.shape[1:]))


def solution(mesh):
    placed = (P(None, None, "chan", "tm"), P("tm", "chan"), P("tm", "chan"))
    return jax.shard_map(
        shards,
        mesh=mesh,
        in_specs=placed,
        out_specs=P(("chan", "tm"), None, None, None),
        check_vma=False,
    )
```

time: 99.9 us -> 84.6 us (0.85)
  blocking collectives: 0 us -> 76.4 us
  waiting for transfers between devices: 55 us -> 0 us
  starting transfers between devices: 21.2 us -> 0 us
  local copies, waits for them, and re-layouts: 13.8 us -> 0 us
  Pallas kernels: 0 us -> 7.99 us
  other arithmetic: 5.65 us -> 0 us
  matrix products: 3.88 us -> 0 us
    all_to_all x0 -> x1, blocking collectives: none -> 76.4 us  [shards(): line = lax.all_to_all(line, ('chan', 'tm'), 0, 0, tiled=True)]
    all_to_all x1 -> x0, waiting for transfers between devices: 55 us -> none  [shards(): line = lax.all_to_all(line, ('chan', 'tm'), 0, 0, tiled=True)]
    all_to_all x1 -> x0, starting transfers between devices: 21.2 us -> none  [shards(): line = lax.all_to_all(line, ('chan', 'tm'), 0, 0, tiled=True)]
    pallas_call x0 -> x2, Pallas kernels: none -> 7.99 us  [the longest x1 4.71 us: gram(): pl.pallas_call(gram_kernel, in_specs=[pl.BlockSpec(memory_space=pl.ANY)],...]
    reshape x2 -> x0, local copies, waits for them, and re-layouts: 4.34 us -> none  [the longest x1 2.19 us: shards(): line = line.reshape(chan_devices, time_devices, parts, ants, times)]
    another operation x2 -> x0, local copies, waits for them, and re-layouts: 3.91 us -> none  [the longest x1 2.32 us: shards(): line = line.reshape(parts, chan_devices * ants, -1)]
    dot_general x4 -> x0, matrix products: 3.88 us -> none  [gram(): return jnp.einsum('it,jt->ij', a, b, preferred_element_type=jnp.float32)]
    another operation x2 -> x0, other arithmetic: 2.73 us -> none  [the longest x1 2.69 us: shards(): line = jnp.stack([real_part, voltages[1]], axis=1)]
  transfers between devices with their start and end apart: 1 -> 0, of which waited for: 1 -> 0; matrix products, arithmetic and copies ran while one was open for 0% -> 0% of each run, Pallas kernels for 0% -> 0%
where the time goes in v3:
time: 84.6 us; the launch traced here: 84.4 us
  blocking collectives  76.4 us (90%)
  Pallas kernels  7.99 us (9%)
    all_to_all x1, blocking collectives, shards(): line = lax.all_to_all(line, ('chan', 'tm'), 0, 0, tiled=True)  76.4 us
    pallas_call x1, Pallas kernels, gram(): pl.pallas_call(gram_kernel, in_specs=[pl.BlockSpec(memory_space=pl.ANY)],...  4.71 us
    pallas_call x1, Pallas kernels, pack(): pl.pallas_call(pack_kernel, in_specs=[pl.BlockSpec(memory_space=pltpu.SME...  3.28 us

profile of v3, /device:TPU:2, one launch (start us, length us, event | category | flops | bytes accessed | tf_op | source)
XLA Modules:
  0.0 84.4 jit_solution(12498985642301383593)
XLA Ops:
  0.0 3.3 %pack.1 = bf16[512,2,4,256]{3,2,1,0:T(4,128)(2,1)} custom-call(s32[2,4]{1,0:T(2,128)} %mask_ref.1, s32[2,4]{1,0:T(2,128)} %count_ref.1, bf16[2,512,4,256]{3,2,1,0:T(4,128)(2,1)} %volt_ref.1), custom_call_target="tpu_custom_call" | custom-call | tf_op jit(solution)/shard_map/pack/pallas_call | solution.py:55
  3.3 76.4 %all_to_all.5 = bf16[512,2,4,256]{3,2,1,0:T(4,128)(2,1)} all-to-all(bf16[512,2,4,256]{3,2,1,0:T(4,128)(2,1)} %pack.1), channel_id=1, replica_groups=mesh['chan'=64,'tm'=8] {'chan','tm'}, dimensions={0} | all-to-all | bytes 4194304 | tf_op jit(solution)/shard_map/all_to_all | solution.py:134
  79.7 4.7 %gram.1 = f32[1,2,256,256]{3,2,1,0:T(8,128)} custom-call(bf16[64,8,2,4,256]{4,3,2,1,0:T(4,128)(2,1)} %bitcast.1), custom_call_target="tpu_custom_call" | custom-call | tf_op jit(solution)/shard_map/gram/pallas_call | solution.py:115

commit v4 on v3

--- a/solution.py
+++ b/solution.py
@@ -9,6 +9,7 @@
 CODE_FLOOR = 8.0
 CODE_BASE = 16.0
 PACK_CHUNKS = 4
+GRAM_TURNS = 2
 
 
 def pack_kernel(mask_ref, count_ref, volt_ref, out_ref, scr, in_sem, out_sem):
@@ -70,61 +71,78 @@
     )(flag_mask, counts, voltages)
 
 
-def gram_kernel(line_ref, out_ref, line_scr, volt_scr, keep_scr, sem):
-    groups, times_devices, parts, ants, times = line_ref.shape
+def gram_kernel(line_ref, out_ref, volt_scr, keep_scr, out_scr, sem):
+    groups, time_devices, _, ants, times = line_ref.shape
     blocks = times // WIDTH
     all_ants = groups * ants
-    samples = times_devices * times
-
-    def into(t):
-        return pltpu.make_async_copy(line_ref.at[:, t], line_scr.at[t], sem.at[t])
-
-    for t in range(times_devices):
-        into(t).start()
     lane = lax.broadcasted_iota(jnp.int32, (all_ants, WIDTH), 1).astype(jnp.float32)
-    for t in range(times_devices):
-        into(t).wait()
-        for b in range(blocks):
-            def piece(p):
-                x = line_scr[t, :, p, :, b * WIDTH : (b + 1) * WIDTH]
-                return x.astype(jnp.float32).reshape(all_ants, WIDTH)
-
-            re, im = piece(0), piece(1)
-            head = re[:, 0:1]
-            keep = lane >= jnp.where(head > CODE_FLOOR, head - CODE_BASE, 0.0)
-            at = t * times + b * WIDTH
-            end = at + WIDTH
-            volt_scr[:, at:end] = jnp.where(keep, re, 0.0).astype(volt_scr.dtype)
-            volt_scr[:, samples + at : samples + end] = jnp.where(keep, im, 0.0).astype(volt_scr.dtype)
-            keep_scr[:, at:end] = jnp.where(keep, 1.0, 0.0).astype(keep_scr.dtype)
 
     def dot(a, b):
         return lax.dot_general(a, b, (((1,), (1,)), ((), ())), preferred_element_type=jnp.float32)
 
-    both, keep = volt_scr[...], keep_scr[...]
-    scale = 1.0 / jnp.maximum(dot(keep, keep), 1.0)
-    out_ref[0, 0] = dot(both, both) * scale
-    cross = dot(both[:, samples:], both[:, :samples])
-    out_ref[0, 1] = (cross - cross.T) * scale
+    def out(p):
+        return pltpu.make_async_copy(out_scr.at[p], out_ref.at[0, p], sem.at[p])
+
+    sums = None
+    share = time_devices // GRAM_TURNS
+    samples = share * times
+    for turn in range(GRAM_TURNS):
+        for t in range(share):
+            for b in range(blocks):
+
+                def piece(p):
+                    x = line_ref[:, turn * share + t, p, :, b * WIDTH : (b + 1) * WIDTH]
+                    return x.astype(jnp.float32).reshape(all_ants, WIDTH)
+
+                re, im = piece(0), piece(1)
+                head = re[:, 0:1]
+                keep = lane >= jnp.where(head > CODE_FLOOR, head - CODE_BASE, 0.0)
+                at = t * times + b * WIDTH
+                end = at + WIDTH
+                volt_scr[turn, :, at:end] = jnp.where(keep, re, 0.0).astype(volt_scr.dtype)
+                volt_scr[turn, :, samples + at : samples + end] = jnp.where(keep, im, 0.0).astype(
+                    volt_scr.dtype
+                )
+                keep_scr[turn, :, at:end] = jnp.where(keep, 1.0, 0.0).astype(keep_scr.dtype)
+        both, keep = volt_scr[turn], keep_scr[turn]
+        last = turn == GRAM_TURNS - 1
+        parts = [lambda: dot(keep, keep), lambda: dot(both, both), lambda: dot(both[:, samples:], both[:, :samples])]
+        if not last:
+            fresh = [f() for f in parts]
+            sums = fresh if sums is None else [x + y for x, y in zip(sums, fresh)]
+        else:
+            old = [0.0] * 3 if sums is None else sums
+            scale = 1.0 / jnp.maximum(parts[0]() + old[0], 1.0)
+            out_scr[0] = (parts[1]() + old[1]) * scale
+            out(0).start()
+            cross = parts[2]() + old[2]
+            out_scr[1] = (cross - cross.T) * scale
+            out(1).start()
+    out(0).wait()
+    out(1).wait()
 
 
 def gram(line):
     groups, time_devices, parts, ants, times = line.shape
     all_ants = groups * ants
-    samples = time_devices * times
+    samples = time_devices * times // GRAM_TURNS
     return pl.pallas_call(
         gram_kernel,
-        in_specs=[pl.BlockSpec(memory_space=pl.ANY)],
-        out_specs=pl.BlockSpec(memory_space=pltpu.VMEM),
+        in_specs=[pl.BlockSpec(memory_space=pltpu.VMEM)],
+        out_specs=pl.BlockSpec(memory_space=pl.ANY),
         out_shape=jax.ShapeDtypeStruct((1, 2, all_ants, all_ants), jnp.float32),
         scratch_shapes=[
-            pltpu.VMEM((time_devices, groups, parts, ants, times), line.dtype),
-            pltpu.VMEM((all_ants, parts * samples), line.dtype),
-            pltpu.VMEM((all_ants, samples), line.dtype),
-            pltpu.SemaphoreType.DMA((time_devices,)),
+            pltpu.VMEM((GRAM_TURNS, all_ants, parts * samples), line.dtype),
+            pltpu.VMEM((GRAM_TURNS, all_ants, samples), line.dtype),
+            pltpu.VMEM((2, all_ants, all_ants), jnp.float32),
+            pltpu.SemaphoreType.DMA((2,)),
         ],
         name="gram",
     )(line)
+
+
+def pin(x):
+    return pltpu.with_memory_space_constraint(x, pltpu.VMEM)
 
 
 def shards(voltages, flag_mask, flagged_prefix_counts):
@@ -132,7 +150,8 @@
     time_devices = lax.axis_size("tm")
     line = pack(voltages, flag_mask, flagged_prefix_counts)
     line = lax.all_to_all(line, ("chan", "tm"), 0, 0, tiled=True)
-    return gram(line.reshape(chan_devices, time_devices, *line.shape[1:]))
+    line = line.reshape(chan_devices, time_devices, *line.shape[1:])
+    return gram(pin(line))
 
 
 def solution(mesh):

time: 84.6 us -> 82.9 us (0.980)
  Pallas kernels: 7.99 us -> 6.44 us
    pallas_call x1, Pallas kernels: 4.71 us -> 3.16 us  [gram(): pl.pallas_call(gram_kernel, in_specs=[pl.BlockSpec(memory_space=pltpu.VME...]
where the time goes in v4:
time: 82.9 us; the launch traced here: 82.7 us
  blocking collectives  76.3 us (92%)
  Pallas kernels  6.44 us (8%)
    all_to_all x1, blocking collectives, shards(): line = lax.all_to_all(line, ('chan', 'tm'), 0, 0, tiled=True)  76.3 us
    pallas_call x1, Pallas kernels, pack(): pl.pallas_call(pack_kernel, in_specs=[pl.BlockSpec(memory_space=pltpu.SME...  3.28 us
    pallas_call x1, Pallas kernels, gram(): pl.pallas_call(gram_kernel, in_specs=[pl.BlockSpec(memory_space=pltpu.VME...  3.16 us

profile of v4, /device:TPU:2, one launch (start us, length us, event | category | flops | bytes accessed | tf_op | source)
XLA Modules:
  0.0 82.7 jit_solution(18388051039334973864)
XLA Ops:
  0.0 3.3 %pack.1 = bf16[512,2,4,256]{3,2,1,0:T(4,128)(2,1)} custom-call(s32[2,4]{1,0:T(2,128)} %mask_ref.1, s32[2,4]{1,0:T(2,128)} %count_ref.1, bf16[2,512,4,256]{3,2,1,0:T(4,128)(2,1)} %volt_ref.1), custom_call_target="tpu_custom_call" | custom-call | tf_op jit(solution)/shard_map/pack/pallas_call | solution.py:56
  3.3 76.3 %all_to_all.5 = bf16[512,2,4,256]{3,2,1,0:T(4,128)(2,1)S(1)} all-to-all(bf16[512,2,4,256]{3,2,1,0:T(4,128)(2,1)} %pack.1), channel_id=1, replica_groups=mesh['chan'=64,'tm'=8] {'chan','tm'}, dimensions={0} | all-to-all | bytes 4194304 | tf_op jit(solution)/shard_map/all_to_all | solution.py:152
  79.6 3.2 %gram.1 = f32[1,2,256,256]{3,2,1,0:T(8,128)} custom-call(bf16[64,8,2,4,256]{4,3,2,1,0:T(4,128)(2,1)S(1)} %bitcast.1), custom_call_target="tpu_custom_call" | custom-call | tf_op jit(solution)/shard_map/gram/pallas_call | solution.py:129

commit v5 on v4

--- a/solution.py
+++ b/solution.py
@@ -1,3 +1,5 @@
+import functools
+
 import jax
 import jax.numpy as jnp
 from jax import lax
@@ -8,25 +10,22 @@
 WIDTH = 128
 CODE_FLOOR = 8.0
 CODE_BASE = 16.0
+VMEM_LIMIT = 24 * 2**20
 PACK_CHUNKS = 4
 GRAM_TURNS = 2
 
 
-def pack_kernel(mask_ref, count_ref, volt_ref, out_ref, scr, in_sem, out_sem):
+def pack_kernel(mask_ref, count_ref, volt_ref, out_ref, in_sem):
     parts, channels, ants, times = volt_ref.shape
     blocks = times // WIDTH
     step = channels // PACK_CHUNKS
 
     def into(c, p):
         at = pl.ds(c * step, step)
-        return pltpu.make_async_copy(volt_ref.at[p, at], scr.at[at, p], in_sem.at[c, p])
+        return pltpu.make_async_copy(volt_ref.at[p, at], out_ref.at[at, p], in_sem.at[c, p])
 
-    def out(c):
-        at = pl.ds(c * step, step)
-        return pltpu.make_async_copy(scr.at[at], out_ref.at[at], out_sem.at[c])
-
-    for c in range(PACK_CHUNKS):
-        for p in range(parts):
+    for p in range(parts):
+        for c in range(PACK_CHUNKS):
             into(c, p).start()
     lane = lax.broadcasted_iota(jnp.int32, (ants, WIDTH), 1)
     row = lax.broadcasted_iota(jnp.int32, (ants, WIDTH), 0)
@@ -40,14 +39,12 @@
         puts.append(put)
         codes.append((code.astype(jnp.float32) + CODE_BASE).astype(jnp.bfloat16))
     for c in range(PACK_CHUNKS):
-        for p in range(parts):
-            into(c, p).wait()
+        into(c, 0).wait()
         for b in range(blocks):
             at = (pl.ds(c * step, step), 0, slice(None), pl.ds(b * WIDTH, WIDTH))
-            scr[at] = jnp.where(puts[b][None] > 0.5, codes[b][None], scr[at])
-        out(c).start()
+            out_ref[at] = jnp.where(puts[b][None] > 0.5, codes[b][None], out_ref[at])
     for c in range(PACK_CHUNKS):
-        out(c).wait()
+        into(c, 1).wait()
 
 
 def pack(voltages, flag_mask, counts):
@@ -58,21 +55,19 @@
         in_specs=[
             pl.BlockSpec(memory_space=pltpu.SMEM),
             pl.BlockSpec(memory_space=pltpu.SMEM),
-            pl.BlockSpec(memory_space=pl.ANY),
+            pl.BlockSpec(memory_space=pltpu.HBM),
         ],
-        out_specs=pl.BlockSpec(memory_space=pl.ANY),
-        out_shape=jax.ShapeDtypeStruct(shape, voltages.dtype),
-        scratch_shapes=[
-            pltpu.VMEM(shape, voltages.dtype),
-            pltpu.SemaphoreType.DMA((PACK_CHUNKS, parts)),
-            pltpu.SemaphoreType.DMA((PACK_CHUNKS,)),
-        ],
+        out_specs=pl.BlockSpec(memory_space=pltpu.VMEM),
+        out_shape=pltpu.VMEM(shape, voltages.dtype),
+        scratch_shapes=[pltpu.SemaphoreType.DMA((PACK_CHUNKS, parts))],
         name="pack",
     )(flag_mask, counts, voltages)
 
 
-def gram_kernel(line_ref, out_ref, volt_scr, keep_scr, out_scr, sem):
-    groups, time_devices, _, ants, times = line_ref.shape
+def gram_kernel(flat_ref, out_ref, volt_scr, keep_scr, out_scr, sem, *, time_devices):
+    parts, ants, times = flat_ref.shape[1:]
+    line_ref = flat_ref.reshape(flat_ref.shape[0] // time_devices, time_devices, parts, ants, times)
+    groups = line_ref.shape[0]
     blocks = times // WIDTH
     all_ants = groups * ants
     lane = lax.broadcasted_iota(jnp.int32, (all_ants, WIDTH), 1).astype(jnp.float32)
@@ -106,28 +101,29 @@
                 keep_scr[turn, :, at:end] = jnp.where(keep, 1.0, 0.0).astype(keep_scr.dtype)
         both, keep = volt_scr[turn], keep_scr[turn]
         last = turn == GRAM_TURNS - 1
-        parts = [lambda: dot(keep, keep), lambda: dot(both, both), lambda: dot(both[:, samples:], both[:, :samples])]
+        sums_of = [lambda: dot(keep, keep), lambda: dot(both, both), lambda: dot(both[:, samples:], both[:, :samples])]
         if not last:
-            fresh = [f() for f in parts]
+            fresh = [f() for f in sums_of]
             sums = fresh if sums is None else [x + y for x, y in zip(sums, fresh)]
         else:
             old = [0.0] * 3 if sums is None else sums
-            scale = 1.0 / jnp.maximum(parts[0]() + old[0], 1.0)
-            out_scr[0] = (parts[1]() + old[1]) * scale
+            scale = 1.0 / jnp.maximum(sums_of[0]() + old[0], 1.0)
+            out_scr[0] = (sums_of[1]() + old[1]) * scale
             out(0).start()
-            cross = parts[2]() + old[2]
+            cross = sums_of[2]() + old[2]
             out_scr[1] = (cross - cross.T) * scale
             out(1).start()
     out(0).wait()
     out(1).wait()
 
 
-def gram(line):
-    groups, time_devices, parts, ants, times = line.shape
+def gram(line, time_devices):
+    groups, parts, ants, times = line.shape
+    groups = groups // time_devices
     all_ants = groups * ants
     samples = time_devices * times // GRAM_TURNS
     return pl.pallas_call(
-        gram_kernel,
+        functools.partial(gram_kernel, time_devices=time_devices),
         in_specs=[pl.BlockSpec(memory_space=pltpu.VMEM)],
         out_specs=pl.BlockSpec(memory_space=pl.ANY),
         out_shape=jax.ShapeDtypeStruct((1, 2, all_ants, all_ants), jnp.float32),
@@ -137,6 +133,7 @@
             pltpu.VMEM((2, all_ants, all_ants), jnp.float32),
             pltpu.SemaphoreType.DMA((2,)),
         ],
+        compiler_params=pltpu.CompilerParams(vmem_limit_bytes=VMEM_LIMIT),
         name="gram",
     )(line)
 
@@ -146,12 +143,10 @@
 
 
 def shards(voltages, flag_mask, flagged_prefix_counts):
-    chan_devices = lax.axis_size("chan")
     time_devices = lax.axis_size("tm")
     line = pack(voltages, flag_mask, flagged_prefix_counts)
     line = lax.all_to_all(line, ("chan", "tm"), 0, 0, tiled=True)
-    line = line.reshape(chan_devices, time_devices, *line.shape[1:])
-    return gram(pin(line))
+    return gram(pin(line), time_devices)
 
 
 def solution(mesh):

time: 82.9 us -> 81.7 us (0.986)
  Pallas kernels: 6.44 us -> 5.44 us
    pallas_call x1, Pallas kernels: 3.28 us -> 2.28 us  [pack(): pl.pallas_call(pack_kernel, in_specs=[pl.BlockSpec(memory_space=pltpu.SME...]
where the time goes in v5:
time: 81.7 us; the launch traced here: 81.5 us
  blocking collectives  76.1 us (93%)
  Pallas kernels  5.44 us (7%)
    all_to_all x1, blocking collectives, shards(): line = lax.all_to_all(line, ('chan', 'tm'), 0, 0, tiled=True)  76.1 us
    pallas_call x1, Pallas kernels, gram(): pl.pallas_call(functools.partial(gram_kernel, time_devices=time_devices),...  3.17 us
    pallas_call x1, Pallas kernels, pack(): pl.pallas_call(pack_kernel, in_specs=[pl.BlockSpec(memory_space=pltpu.SME...  2.28 us

profile of v5, /device:TPU:2, one launch (start us, length us, event | category | flops | bytes accessed | tf_op | source)
XLA Modules:
  0.0 81.5 jit_solution(3223294442242853558)
XLA Ops:
  0.0 2.3 %pack.1 = bf16[512,2,4,256]{3,2,1,0:T(4,128)(2,1)S(1)} custom-call(s32[2,4]{1,0:T(2,128)} %mask_ref.1, s32[2,4]{1,0:T(2,128)} %count_ref.1, bf16[2,512,4,256]{3,2,1,0:T(4,128)(2,1)} %volt_ref.1), custom_call_target="tpu_custom_call" | custom-call | tf_op jit(solution)/shard_map/pack/pallas_call | solution.py:53
  2.3 76.1 %all_to_all.5.flat_ref = bf16[512,2,4,256]{3,2,1,0:T(4,128)(2,1)S(1)} all-to-all(bf16[512,2,4,256]{3,2,1,0:T(4,128)(2,1)S(1)} %pack.1), channel_id=1, replica_groups=mesh['chan'=64,'tm'=8] {'chan','tm'}, dimensions={0} | all-to-all | bytes 4194304 | tf_op jit(solution)/shard_map/all_to_all | solution.py:148
  78.3 3.2 %gram.1 = f32[1,2,256,256]{3,2,1,0:T(8,128)} custom-call(bf16[512,2,4,256]{3,2,1,0:T(4,128)(2,1)S(1)} %all_to_all.5.flat_ref), custom_call_target="tpu_custom_call" | custom-call | tf_op jit(solution)/shard_map/gram/pallas_call | solution.py:125

commit v6 on v5

--- a/solution.py
+++ b/solution.py
@@ -8,11 +8,10 @@
 from jax.sharding import PartitionSpec as P
 
 WIDTH = 128
-CODE_FLOOR = 8.0
 CODE_BASE = 16.0
 VMEM_LIMIT = 24 * 2**20
 PACK_CHUNKS = 4
-GRAM_TURNS = 2
+GRAM_TURNS = 8
 
 
 def pack_kernel(mask_ref, count_ref, volt_ref, out_ref, in_sem):
@@ -70,7 +69,10 @@
     groups = line_ref.shape[0]
     blocks = times // WIDTH
     all_ants = groups * ants
-    lane = lax.broadcasted_iota(jnp.int32, (all_ants, WIDTH), 1).astype(jnp.float32)
+    lane_code = lax.broadcasted_iota(jnp.int32, (all_ants, WIDTH), 1).astype(jnp.float32) + CODE_BASE
+    lane_code = lane_code.astype(jnp.bfloat16)
+    zero = jnp.zeros((), jnp.bfloat16)
+    one = jnp.ones((), jnp.bfloat16)
 
     def dot(a, b):
         return lax.dot_general(a, b, (((1,), (1,)), ((), ())), preferred_element_type=jnp.float32)
@@ -87,18 +89,15 @@
 
                 def piece(p):
                     x = line_ref[:, turn * share + t, p, :, b * WIDTH : (b + 1) * WIDTH]
-                    return x.astype(jnp.float32).reshape(all_ants, WIDTH)
+                    return x.astype(jnp.float32).reshape(all_ants, WIDTH).astype(jnp.bfloat16)
 
                 re, im = piece(0), piece(1)
-                head = re[:, 0:1]
-                keep = lane >= jnp.where(head > CODE_FLOOR, head - CODE_BASE, 0.0)
+                keep = lane_code >= re[:, 0:1]
                 at = t * times + b * WIDTH
                 end = at + WIDTH
-                volt_scr[turn, :, at:end] = jnp.where(keep, re, 0.0).astype(volt_scr.dtype)
-                volt_scr[turn, :, samples + at : samples + end] = jnp.where(keep, im, 0.0).astype(
-                    volt_scr.dtype
-                )
-                keep_scr[turn, :, at:end] = jnp.where(keep, 1.0, 0.0).astype(keep_scr.dtype)
+                volt_scr[turn, :, at:end] = jnp.where(keep, re, zero)
+                volt_scr[turn, :, samples + at : samples + end] = jnp.where(keep, im, zero)
+                keep_scr[turn, :, at:end] = jnp.where(keep, one, zero)
         both, keep = volt_scr[turn], keep_scr[turn]
         last = turn == GRAM_TURNS - 1
         sums_of = [lambda: dot(keep, keep), lambda: dot(both, both), lambda: dot(both[:, samples:], both[:, :samples])]

time: 81.7 us -> 81 us (level)
  no operation moved by 1% of the time
where the time goes in v6:
time: 81 us; the launch traced here: 80.9 us
  blocking collectives  76.1 us (94%)
  Pallas kernels  4.79 us (6%)
    all_to_all x1, blocking collectives, shards(): line = lax.all_to_all(line, ('chan', 'tm'), 0, 0, tiled=True)  76.1 us
    pallas_call x1, Pallas kernels, gram(): pl.pallas_call(functools.partial(gram_kernel, time_devices=time_devices),...  2.51 us
    pallas_call x1, Pallas kernels, pack(): pl.pallas_call(pack_kernel, in_specs=[pl.BlockSpec(memory_space=pltpu.SME...  2.28 us

profile of v6, /device:TPU:2, one launch (start us, length us, event | category | flops | bytes accessed | tf_op | source)
XLA Modules:
  0.0 80.9 jit_solution(15446897915990773066)
XLA Ops:
  0.0 2.3 %pack.1 = bf16[512,2,4,256]{3,2,1,0:T(4,128)(2,1)S(1)} custom-call(s32[2,4]{1,0:T(2,128)} %mask_ref.1, s32[2,4]{1,0:T(2,128)} %count_ref.1, bf16[2,512,4,256]{3,2,1,0:T(4,128)(2,1)} %volt_ref.1), custom_call_target="tpu_custom_call" | custom-call | tf_op jit(solution)/shard_map/pack/pallas_call | solution.py:52
  2.3 76.1 %all_to_all.5.flat_ref = bf16[512,2,4,256]{3,2,1,0:T(4,128)(2,1)S(1)} all-to-all(bf16[512,2,4,256]{3,2,1,0:T(4,128)(2,1)S(1)} %pack.1), channel_id=1, replica_groups=mesh['chan'=64,'tm'=8] {'chan','tm'}, dimensions={0} | all-to-all | bytes 4194304 | tf_op jit(solution)/shard_map/all_to_all | solution.py:147
  78.3 2.5 %gram.1 = f32[1,2,256,256]{3,2,1,0:T(8,128)} custom-call(bf16[512,2,4,256]{3,2,1,0:T(4,128)(2,1)S(1)} %all_to_all.5.flat_ref), custom_call_target="tpu_custom_call" | custom-call | tf_op jit(solution)/shard_map/gram/pallas_call | solution.py:124

commit v7 on v6

v7 whole, which is shorter than its diff:
```python
import functools

import jax
import jax.numpy as jnp
from jax import lax
from jax.experimental import pallas as pl
from jax.experimental.pallas import tpu as pltpu
from jax.sharding import PartitionSpec as P

WIDTH = 128
CODE_BASE = 16.0
VMEM_LIMIT = 24 * 2**20
PACK_CHUNKS = 2
GRAM_TURNS = 8


def pack_kernel(mask_hbm, count_hbm, volt_ref, out_ref, mask_ref, count_ref, in_sem, flag_sem):
    parts, channels, rows, _ = volt_ref.shape
    blocks, ants = mask_ref.shape
    step = channels // PACK_CHUNKS

    def into(c, p):
        at = pl.ds(c * step, step)
        return pltpu.make_async_copy(volt_ref.at[p, at], out_ref.at[at, p], in_sem.at[c, p])

    flags = [
        pltpu.make_async_copy(mask_hbm, mask_ref, flag_sem.at[0]),
        pltpu.make_async_copy(count_hbm, count_ref, flag_sem.at[1]),
    ]
    for copy in flags:
        copy.start()
    for p in range(parts):
        for c in range(PACK_CHUNKS):
            into(c, p).start()
    for copy in flags:
        copy.wait()
    lane = lax.broadcasted_iota(jnp.int32, (rows, WIDTH), 1)
    row = lax.broadcasted_iota(jnp.int32, (rows, WIDTH), 0)
    code = jnp.zeros((rows, WIDTH), jnp.int32)
    for b in range(blocks):
        for a in range(ants):
            first = jnp.where(mask_ref[b, a] == 1, count_ref[b, a], WIDTH)
            code = jnp.where(row == b * ants + a, first, code)
    put = jnp.where((lane == 0) & (code > 0), 1.0, 0.0).astype(jnp.bfloat16)
    code = (code.astype(jnp.float32) + CODE_BASE).astype(jnp.bfloat16)
    for c in range(PACK_CHUNKS):
        into(c, 0).wait()
        at = (pl.ds(c * step, step), 0)
        out_ref[at] = jnp.where(put[None] > 0.5, code[None], out_ref[at])
    for c in range(PACK_CHUNKS):
        into(c, 1).wait()


def pack(voltages, flag_mask, counts):
    parts, channels, ants, times = voltages.shape
    blocks = times // WIDTH
    tiles = voltages.reshape(parts, channels, ants, blocks, WIDTH).transpose(0, 1, 3, 2, 4)
    tiles = tiles.reshape(parts, channels, blocks * ants, WIDTH)
    return pl.pallas_call(
        pack_kernel,
        in_specs=[
            pl.BlockSpec(memory_space=pltpu.HBM),
            pl.BlockSpec(memory_space=pltpu.HBM),
            pl.BlockSpec(memory_space=pltpu.HBM),
        ],
        out_specs=pl.BlockSpec(memory_space=pltpu.VMEM),
        out_shape=pltpu.VMEM((channels, parts, blocks * ants, WIDTH), voltages.dtype),
        scratch_shapes=[
            pltpu.SMEM(flag_mask.shape, flag_mask.dtype),
            pltpu.SMEM(counts.shape, counts.dtype),
            pltpu.SemaphoreType.DMA((PACK_CHUNKS, parts)),
            pltpu.SemaphoreType.DMA((2,)),
        ],
        name="pack",
    )(flag_mask, counts, tiles)


def gram_kernel(flat_ref, out_ref, volt_scr, keep_scr, out_scr, sem, *, time_devices, ants):
    parts, rows, _ = flat_ref.shape[1:]
    groups = flat_ref.shape[0] // time_devices
    line_ref = flat_ref.reshape(groups, time_devices, parts, rows, WIDTH)
    blocks = rows // ants
    all_ants = groups * ants
    lane_code = lax.broadcasted_iota(jnp.int32, (all_ants, WIDTH), 1).astype(jnp.float32) + CODE_BASE
    lane_code = lane_code.astype(jnp.bfloat16)
    upper = lax.broadcasted_iota(jnp.int32, (1, rows, WIDTH), 1) >= ants
    zero = jnp.zeros((), jnp.bfloat16)
    one = jnp.ones((), jnp.bfloat16)

    def dot(a, b):
        return lax.dot_general(a, b, (((1,), (1,)), ((), ())), preferred_element_type=jnp.float32)

    def out(p):
        return pltpu.make_async_copy(out_scr.at[p], out_ref.at[0, p], sem.at[p])

    def pieces(t, p):
        x = line_ref[:, t, p].astype(jnp.float32).reshape(groups // 2, 2, rows, WIDTH)
        even, odd = x[:, 0], x[:, 1]
        first = jnp.where(upper, pltpu.roll(odd, ants, 1), even)
        second = jnp.where(upper, odd, pltpu.roll(even, ants, 1))
        return [y.reshape(all_ants, WIDTH).astype(jnp.bfloat16) for y in (first, second)]

    sums = None
    share = time_devices // GRAM_TURNS
    samples = share * blocks * WIDTH
    for turn in range(GRAM_TURNS):
        for t in range(share):
            reals, imags = pieces(turn * share + t, 0), pieces(turn * share + t, 1)
            for b in range(blocks):
                re, im = reals[b], imags[b]
                keep = lane_code >= re[:, 0:1]
                at = (t * blocks + b) * WIDTH
                end = at + WIDTH
                volt_scr[turn, :, at:end] = jnp.where(keep, re, zero)
                volt_scr[turn, :, samples + at : samples + end] = jnp.where(keep, im, zero)
                keep_scr[turn, :, at:end] = jnp.where(keep, one, zero)
        both, keep = volt_scr[turn], keep_scr[turn]
        last = turn == GRAM_TURNS - 1
        sums_of = [lambda: dot(keep, keep), lambda: dot(both, both), lambda: dot(both[:, samples:], both[:, :samples])]
        if not last:
            fresh = [f() for f in sums_of]
            sums = fresh if sums is None else [x + y for x, y in zip(sums, fresh)]
        else:
            old = [0.0] * 3 if sums is None else sums
            scale = 1.0 / jnp.maximum(sums_of[0]() + old[0], 1.0)
            out_scr[0] = (sums_of[1]() + old[1]) * scale
            out(0).start()
            cross = sums_of[2]() + old[2]
            out_scr[1] = (cross - cross.T) * scale
            out(1).start()
    out(0).wait()
    out(1).wait()


def gram(line, time_devices, ants):
    senders, parts, rows, _ = line.shape
    groups = senders // time_devices
    all_ants = groups * ants
    samples = time_devices // GRAM_TURNS * rows // ants * WIDTH
    return pl.pallas_call(
        functools.partial(gram_kernel, time_devices=time_devices, ants=ants),
        in_specs=[pl.BlockSpec(memory_space=pltpu.VMEM)],
        out_specs=pl.BlockSpec(memory_space=pl.ANY),
        out_shape=jax.ShapeDtypeStruct((1, 2, all_ants, all_ants), jnp.float32),
        scratch_shapes=[
            pltpu.VMEM((GRAM_TURNS, all_ants, parts * samples), line.dtype),
            pltpu.VMEM((GRAM_TURNS, all_ants, samples), line.dtype),
            pltpu.VMEM((2, all_ants, all_ants), jnp.float32),
            pltpu.SemaphoreType.DMA((2,)),
        ],
        compiler_params=pltpu.CompilerParams(vmem_limit_bytes=VMEM_LIMIT),
        name="gram",
    )(line)


def pin(x):
    return pltpu.with_memory_space_constraint(x, pltpu.VMEM)


def shards(voltages, flag_mask, flagged_prefix_counts):
    time_devices = lax.axis_size("tm")
    line = pack(voltages, flag_mask, flagged_prefix_counts)
    line = lax.all_to_all(line, ("chan", "tm"), 0, 0, tiled=True)
    return gram(pin(line), time_devices, voltages.shape[2])


def solution(mesh):
    placed = (P(None, None, "chan", "tm"), P("tm", "chan"), P("tm", "chan"))
    return jax.shard_map(
        shards,
        mesh=mesh,
        in_specs=placed,
        out_specs=P(("chan", "tm"), None, None, None),
        check_vma=False,
    )
```

time: 81 us -> 80.2 us (level)
  no operation moved by 1% of the time
where the time goes in v7:
time: 80.2 us; the launch traced here: 80.1 us
  blocking collectives  76.1 us (95%)
  Pallas kernels  4.02 us (5%)
    all_to_all x1, blocking collectives, shards(): line = lax.all_to_all(line, ('chan', 'tm'), 0, 0, tiled=True)  76.1 us
    pallas_call x1, Pallas kernels, gram(): pl.pallas_call(functools.partial(gram_kernel, time_devices=time_devices,...  2.45 us

profile of v7, /device:TPU:2, one launch (start us, length us, event | category | flops | bytes accessed | tf_op | source)
XLA Modules:
  0.0 80.1 jit_solution(4843606776876529759)
XLA Ops:
  0.0 1.6 %pack.1 = bf16[512,2,8,128]{3,2,1,0:T(8,128)(2,1)S(1)} custom-call(s32[2,4]{1,0:T(2,128)} %mask_hbm.1, s32[2,4]{1,0:T(2,128)} %count_hbm.1, bf16[2,512,8,128]{3,2,1,0:T(8,128)(2,1)} %bitcast.5), custom_call_target="tpu_custom_call" | custom-call | tf_op jit(solution)/shard_map/pack/pallas_call | solution.py:59
  1.6 76.1 %all_to_all.5.flat_ref = bf16[512,2,8,128]{3,2,1,0:T(8,128)(2,1)S(1)} all-to-all(bf16[512,2,8,128]{3,2,1,0:T(8,128)(2,1)S(1)} %pack.1), channel_id=1, replica_groups=mesh['chan'=64,'tm'=8] {'chan','tm'}, dimensions={0} | all-to-all | bytes 4194304 | tf_op jit(solution)/shard_map/all_to_all | solution.py:163
  77.6 2.5 %gram.1 = f32[1,2,256,256]{3,2,1,0:T(8,128)} custom-call(bf16[512,2,8,128]{3,2,1,0:T(8,128)(2,1)S(1)} %all_to_all.5.flat_ref), custom_call_target="tpu_custom_call" | custom-call | tf_op jit(solution)/shard_map/gram/pallas_call | solution.py:140

commit v8 on v7

--- a/solution.py
+++ b/solution.py
@@ -83,7 +83,6 @@
     all_ants = groups * ants
     lane_code = lax.broadcasted_iota(jnp.int32, (all_ants, WIDTH), 1).astype(jnp.float32) + CODE_BASE
     lane_code = lane_code.astype(jnp.bfloat16)
-    upper = lax.broadcasted_iota(jnp.int32, (1, rows, WIDTH), 1) >= ants
     zero = jnp.zeros((), jnp.bfloat16)
     one = jnp.ones((), jnp.bfloat16)
 
@@ -94,11 +93,14 @@
         return pltpu.make_async_copy(out_scr.at[p], out_ref.at[0, p], sem.at[p])
 
     def pieces(t, p):
-        x = line_ref[:, t, p].astype(jnp.float32).reshape(groups // 2, 2, rows, WIDTH)
-        even, odd = x[:, 0], x[:, 1]
-        first = jnp.where(upper, pltpu.roll(odd, ants, 1), even)
-        second = jnp.where(upper, odd, pltpu.roll(even, ants, 1))
-        return [y.reshape(all_ants, WIDTH).astype(jnp.bfloat16) for y in (first, second)]
+        x = line_ref[:, t, p].reshape(groups // 2, 2 * rows, WIDTH)
+
+        def joined(b):
+            near, far = b * ants, rows + b * ants
+            pair = (x[:, near : near + ants], x[:, far : far + ants])
+            return jnp.concatenate(pair, axis=1).reshape(all_ants, WIDTH)
+
+        return [joined(b) for b in range(blocks)]
 
     sums = None
     share = time_devices // GRAM_TURNS

time: 80.2 us -> 80.1 us (level)
  no operation moved by 1% of the time
where the time goes in v8:
time: 80.1 us; the launch traced here: 80 us
  blocking collectives  76.1 us (95%)
  Pallas kernels  3.92 us (5%)
    all_to_all x1, blocking collectives, shards(): line = lax.all_to_all(line, ('chan', 'tm'), 0, 0, tiled=True)  76.1 us
    pallas_call x1, Pallas kernels, gram(): pl.pallas_call(functools.partial(gram_kernel, time_devices=time_devices,...  2.35 us

profile of v8, /device:TPU:2, one launch (start us, length us, event | category | flops | bytes accessed | tf_op | source)
XLA Modules:
  0.0 80.0 jit_solution(3646435393733641110)
XLA Ops:
  0.0 1.6 %pack.1 = bf16[512,2,8,128]{3,2,1,0:T(8,128)(2,1)S(1)} custom-call(s32[2,4]{1,0:T(2,128)} %mask_hbm.1, s32[2,4]{1,0:T(2,128)} %count_hbm.1, bf16[2,512,8,128]{3,2,1,0:T(8,128)(2,1)} %bitcast.5), custom_call_target="tpu_custom_call" | custom-call | tf_op jit(solution)/shard_map/pack/pallas_call | solution.py:59
  1.6 76.1 %all_to_all.5.flat_ref = bf16[512,2,8,128]{3,2,1,0:T(8,128)(2,1)S(1)} all-to-all(bf16[512,2,8,128]{3,2,1,0:T(8,128)(2,1)S(1)} %pack.1), channel_id=1, replica_groups=mesh['chan'=64,'tm'=8] {'chan','tm'}, dimensions={0} | all-to-all | bytes 4194304 | tf_op jit(solution)/shard_map/all_to_all | solution.py:165
  77.6 2.4 %gram.1 = f32[1,2,256,256]{3,2,1,0:T(8,128)} custom-call(bf16[512,2,8,128]{3,2,1,0:T(8,128)(2,1)S(1)} %all_to_all.5.flat_ref), custom_call_target="tpu_custom_call" | custom-call | tf_op jit(solution)/shard_map/gram/pallas_call | solution.py:142
